TPU v7x, 32 devices: a whole 2x2x4 slice. The times are simulated.
32 devices in a mesh: dp: 8 (over y, x, core), tensor: 4 (over z).
Axes of the slice: x: 2, y: 2, z: 4, core: 2. Of those that a mesh axis runs over, the one named last changes fastest.
Arguments:
- activations: bfloat16 [8, 1024, 1536], P('dp', 'tensor'), may hold values from -6 to 6
- lengths: int32 [8], P('dp'), may hold values from 256 to 1024, as said below
- attn_gain: bfloat16 [1536], P('dp'), may hold values from 0.5 to 1.5
- w_query: bfloat16 [1536, 1536], P('dp', 'tensor'), may hold values from -0.15625 to 0.15625
- w_key: bfloat16 [1536, 768], P('dp', 'tensor'), may hold values from -0.15625 to 0.15625
- w_value: bfloat16 [1536, 768], P('dp', 'tensor'), may hold values from -0.15625 to 0.15625
- w_out: bfloat16 [1536, 1536], P('tensor', 'dp'), may hold values from -3 to 3
- mlp_gain: bfloat16 [1536], P('dp'), may hold values from 0.5 to 1.5
- w_gate: bfloat16 [1536, 4096], P('dp', 'tensor'), may hold values from -0.15625 to 0.15625
- w_up: bfloat16 [1536, 4096], P('dp', 'tensor'), may hold values from -0.15625 to 0.15625
- w_down: bfloat16 [4096, 1536], P('tensor', 'dp'), may hold values from -0.09375 to 0.09375
- cotangent: bfloat16 [8, 1024, 1536], P('dp', 'tensor'), may hold values from -6 to 6
Outputs:
- out_acts: float32 [8, 1024, 1536], P('dp', 'tensor')
- grad_acts: float32 [8, 1024, 1536], P('dp', 'tensor')
- grad_attn_gain: float32 [1536], P('dp')
- grad_query: float32 [1536, 1536], P('dp', 'tensor')
- grad_key: float32 [1536, 768], P('dp', 'tensor')
- grad_value: float32 [1536, 768], P('dp', 'tensor')
- grad_out: float32 [1536, 1536], P('tensor', 'dp')
- grad_mlp_gain: float32 [1536], P('dp')
- grad_gate: float32 [1536, 4096], P('dp', 'tensor')
- grad_up: float32 [1536, 4096], P('dp', 'tensor')
- grad_down: float32 [4096, 1536], P('tensor', 'dp')
Inputs may be any that keep to these rules, and one draw needn't show every extreme that they name: `lengths`: valid slots of each sequence; in every draw one sequence is full (1024) and one has exactly 256.
All inputs are finite; a program needn't handle non-finite values.
Results may differ from a plain program's by a relative error of at most 0.017.
Values may be sent and summed in bfloat16 or wider, within the bound.
A program may use at most 192 MiB of HBM per device.

v0:
```python
import math
import jax
import jax.numpy as jnp
from jax import lax
from jax.sharding import PartitionSpec as P

HEAD_DIM = 96
EPS = 1e-05
THETA = 100000.0
NEG = -1e30


def rope_tables(count, width):
    half = width // 2
    freqs = THETA ** (-jnp.arange(half, dtype=jnp.float32) * (2.0 / width))
    angles = jnp.arange(count, dtype=jnp.float32)[:, None] * freqs[None, :]
    return (jnp.cos(angles), jnp.sin(angles))


def rotate(vectors, cosines, sines):
    half = vectors.shape[-1] // 2
    first = vectors[..., :half]
    second = vectors[..., half:]
    cos_b = cosines[:, None, :]
    sin_b = sines[:, None, :]
    return jnp.concatenate(
        [first * cos_b - second * sin_b, second * cos_b + first * sin_b], axis=-1
    )


def unrotate(grads, cosines, sines):
    half = grads.shape[-1] // 2
    first = grads[..., :half]
    second = grads[..., half:]
    cos_b = cosines[:, None, :]
    sin_b = sines[:, None, :]
    return jnp.concatenate(
        [first * cos_b + second * sin_b, second * cos_b - first * sin_b], axis=-1
    )


def transposed(left, right):
    return lax.dot_general(
        left, right, (((1,), (1,)), ((), ())), preferred_element_type=jnp.float32
    )


def outer_sum(left, right):
    return lax.dot_general(
        left, right, (((0,), (0,)), ((), ())), preferred_element_type=jnp.float32
    )


def rms_back(grad_norm, normed, inverse):
    return inverse * (grad_norm - normed * jnp.mean(grad_norm * normed, axis=1, keepdims=True))


def scores_block(query_block, key_prefix, start, seq_positions, key_valid, scale):
    block = query_block.shape[0]
    stop = key_prefix.shape[0]
    raw = (
        jnp.einsum("qcgd,kcd->cgqk", query_block, key_prefix, preferred_element_type=jnp.float32)
        * scale
    )
    rows = start + jnp.arange(block)
    allowed = (seq_positions[None, :stop] <= rows[:, None]) & key_valid[None, :stop]
    return jnp.where(allowed, raw, NEG)


def body(
    activations,
    lengths,
    attn_gain,
    w_query,
    w_key,
    w_value,
    w_out,
    mlp_gain,
    w_gate,
    w_up,
    w_down,
    cotangent,
):
    tensor_size = lax.axis_size("tensor")
    tensor_rank = lax.axis_index("tensor")
    tokens = activations[0].astype(jnp.float32)
    local = tokens.shape[0]
    seq_len = local * tensor_size
    length = lengths[0]
    own_valid = (tensor_rank * local + jnp.arange(local) < length)[:, None]
    seq_positions = jnp.arange(seq_len)
    key_valid = seq_positions < length
    cosines, sines = rope_tables(seq_len, HEAD_DIM)
    scale = 1.0 / math.sqrt(HEAD_DIM)
    query_full, key_full, value_full, out_full, first_gain = (
        lax.all_gather(w_query, "dp", axis=0, tiled=True),
        lax.all_gather(w_key, "dp", axis=0, tiled=True),
        lax.all_gather(w_value, "dp", axis=0, tiled=True),
        lax.all_gather(w_out, "dp", axis=1, tiled=True),
        lax.all_gather(attn_gain, "dp", axis=0, tiled=True),
    )
    heads = query_full.shape[1] // HEAD_DIM
    kv_local = key_full.shape[1] // HEAD_DIM
    groups = heads // kv_local
    first_gain_f = first_gain.astype(jnp.float32)
    inv_first = lax.rsqrt(jnp.mean(tokens * tokens, axis=1, keepdims=True) + EPS)
    normed_first = tokens * inv_first
    first_low = (normed_first * first_gain_f).astype(jnp.bfloat16)
    first_all = lax.all_gather(first_low, "tensor", axis=0, tiled=True)
    query_proj = jnp.dot(first_all, query_full, preferred_element_type=jnp.float32).reshape(
        seq_len, heads, HEAD_DIM
    )
    queries = (
        rotate(query_proj, cosines, sines)
        .astype(jnp.bfloat16)
        .reshape(seq_len, kv_local, groups, HEAD_DIM)
    )
    key_proj = jnp.dot(first_all, key_full, preferred_element_type=jnp.float32).reshape(
        seq_len, kv_local, HEAD_DIM
    )
    keys = rotate(key_proj, cosines, sines).astype(jnp.bfloat16)
    values = (
        jnp.dot(first_all, value_full, preferred_element_type=jnp.float32)
        .astype(jnp.bfloat16)
        .reshape(seq_len, kv_local, HEAD_DIM)
    )
    block = min(512, seq_len)
    count = seq_len // block
    pieces = []
    log_sums = []
    for index in range(count):
        start = index * block
        stop = start + block
        scores = scores_block(
            queries[start:stop], keys[:stop], start, seq_positions, key_valid, scale
        )
        peak = jnp.max(scores, axis=3, keepdims=True)
        log_sum = peak + jnp.log(jnp.sum(jnp.exp(scores - peak), axis=3, keepdims=True))
        probs = jnp.exp(scores - log_sum)
        mixed = jnp.einsum(
            "cgqk,kcd->qcgd",
            probs.astype(jnp.bfloat16),
            values[:stop],
            preferred_element_type=jnp.float32,
        )
        pieces.append(mixed.reshape(block, heads * HEAD_DIM))
        log_sums.append(log_sum)
    attended = jnp.concatenate(pieces, axis=0).astype(jnp.bfloat16)
    branch = lax.psum_scatter(
        jnp.dot(attended, out_full, preferred_element_type=jnp.float32),
        "tensor",
        scatter_dimension=0,
        tiled=True,
    )
    middle = tokens + branch
    gate_full, up_full, down_full, second_gain = (
        lax.all_gather(w_gate, "dp", axis=0, tiled=True),
        lax.all_gather(w_up, "dp", axis=0, tiled=True),
        lax.all_gather(w_down, "dp", axis=1, tiled=True),
        lax.all_gather(mlp_gain, "dp", axis=0, tiled=True),
    )
    second_gain_f = second_gain.astype(jnp.float32)
    inv_second = lax.rsqrt(jnp.mean(middle * middle, axis=1, keepdims=True) + EPS)
    normed_second = middle * inv_second
    second_low = (normed_second * second_gain_f).astype(jnp.bfloat16)
    second_all = lax.all_gather(second_low, "tensor", axis=0, tiled=True)
    gate = jnp.dot(second_all, gate_full, preferred_element_type=jnp.float32)
    up_part = jnp.dot(second_all, up_full, preferred_element_type=jnp.float32)
    sigmoid_gate = jax.nn.sigmoid(gate)
    hidden = (gate * sigmoid_gate * up_part).astype(jnp.bfloat16)
    result = middle + lax.psum_scatter(
        jnp.dot(hidden, down_full, preferred_element_type=jnp.float32).astype(jnp.bfloat16),
        "tensor",
        scatter_dimension=0,
        tiled=True,
    ).astype(jnp.float32)
    output = jnp.where(own_valid, result, 0.0)
    query_full, key_full, value_full, out_full, gate_full, up_full, down_full = (
        lax.all_gather(w_query, "dp", axis=0, tiled=True),
        lax.all_gather(w_key, "dp", axis=0, tiled=True),
        lax.all_gather(w_value, "dp", axis=0, tiled=True),
        lax.all_gather(w_out, "dp", axis=1, tiled=True),
        lax.all_gather(w_gate, "dp", axis=0, tiled=True),
        lax.all_gather(w_up, "dp", axis=0, tiled=True),
        lax.all_gather(w_down, "dp", axis=1, tiled=True),
    )
    grad_result = jnp.where(own_valid, cotangent[0].astype(jnp.float32), 0.0)
    grad_mlp_all = lax.all_gather(grad_result.astype(jnp.bfloat16), "tensor", axis=0, tiled=True)
    grad_down_w = outer_sum(hidden, grad_mlp_all)
    grad_hidden = transposed(grad_mlp_all, down_full)
    grad_gate_low = (
        grad_hidden * up_part * sigmoid_gate * (1.0 + gate * (1.0 - sigmoid_gate))
    ).astype(jnp.bfloat16)
    grad_up_low = (grad_hidden * gate * sigmoid_gate).astype(jnp.bfloat16)
    grad_second = lax.psum_scatter(
        transposed(grad_gate_low, gate_full) + transposed(grad_up_low, up_full),
        "tensor",
        scatter_dimension=0,
        tiled=True,
    )
    grad_gate_w = outer_sum(second_all, grad_gate_low)
    grad_up_w = outer_sum(second_all, grad_up_low)
    grad_gate_w, grad_up_w, grad_down_w = (
        lax.psum_scatter(
            grad_gate_w.astype(jnp.bfloat16), "dp", scatter_dimension=0, tiled=True
        ).astype(jnp.float32),
        lax.psum_scatter(
            grad_up_w.astype(jnp.bfloat16), "dp", scatter_dimension=0, tiled=True
        ).astype(jnp.float32),
        lax.psum_scatter(
            grad_down_w.astype(jnp.bfloat16), "dp", scatter_dimension=1, tiled=True
        ).astype(jnp.float32),
    )
    second_gain_part = jnp.sum(grad_second * normed_second, axis=0)
    grad_middle = grad_result + rms_back(grad_second * second_gain_f, normed_second, inv_second)
    grad_attn_all = lax.all_gather(grad_middle.astype(jnp.bfloat16), "tensor", axis=0, tiled=True)
    grad_attended = transposed(grad_attn_all, out_full).astype(jnp.bfloat16)
    grad_out_w = outer_sum(attended, grad_attn_all)
    grad_queries = []
    grad_keys = jnp.zeros((seq_len, kv_local, HEAD_DIM), jnp.float32)
    grad_values = jnp.zeros((seq_len, kv_local, HEAD_DIM), jnp.float32)
    for index in range(count):
        start = index * block
        stop = start + block
        query_block = queries[start:stop]
        scores = scores_block(query_block, keys[:stop], start, seq_positions, key_valid, scale)
        probs = jnp.exp(scores - log_sums[index])
        grad_block = grad_attended[start:stop].reshape(block, kv_local, groups, HEAD_DIM)
        grad_probs = jnp.einsum(
            "qcgd,kcd->cgqk", grad_block, values[:stop], preferred_element_type=jnp.float32
        )
        row_dot = jnp.sum(probs * grad_probs, axis=3, keepdims=True)
        grad_scores = (probs * (grad_probs - row_dot)).astype(jnp.bfloat16)
        query_grad = (
            jnp.einsum(
                "cgqk,kcd->qcgd", grad_scores, keys[:stop], preferred_element_type=jnp.float32
            )
            * scale
        )
        grad_queries.append(query_grad.reshape(block, heads, HEAD_DIM))
        key_grad = (
            jnp.einsum(
                "cgqk,qcgd->kcd", grad_scores, query_block, preferred_element_type=jnp.float32
            )
            * scale
        )
        grad_keys = grad_keys.at[:stop].add(key_grad)
        value_grad = jnp.einsum(
            "cgqk,qcgd->kcd",
            probs.astype(jnp.bfloat16),
            grad_block,
            preferred_element_type=jnp.float32,
        )
        grad_values = grad_values.at[:stop].add(value_grad)
    grad_query_proj = (
        unrotate(jnp.concatenate(grad_queries, axis=0), cosines, sines)
        .astype(jnp.bfloat16)
        .reshape(seq_len, heads * HEAD_DIM)
    )
    grad_key_proj = (
        unrotate(grad_keys, cosines, sines)
        .astype(jnp.bfloat16)
        .reshape(seq_len, kv_local * HEAD_DIM)
    )
    grad_value_proj = grad_values.astype(jnp.bfloat16).reshape(seq_len, kv_local * HEAD_DIM)
    grad_first = lax.psum_scatter(
        (
            transposed(grad_query_proj, query_full)
            + transposed(grad_key_proj, key_full)
            + transposed(grad_value_proj, value_full)
        ).astype(jnp.bfloat16),
        "tensor",
        scatter_dimension=0,
        tiled=True,
    ).astype(jnp.float32)
    grad_query_w = outer_sum(first_all, grad_query_proj)
    grad_key_w = outer_sum(first_all, grad_key_proj)
    grad_value_w = outer_sum(first_all, grad_value_proj)
    grad_query_w, grad_key_w, grad_value_w, grad_out_w = (
        lax.psum_scatter(
            grad_query_w.astype(jnp.bfloat16), "dp", scatter_dimension=0, tiled=True
        ).astype(jnp.float32),
        lax.psum_scatter(
            grad_key_w.astype(jnp.bfloat16), "dp", scatter_dimension=0, tiled=True
        ).astype(jnp.float32),
        lax.psum_scatter(
            grad_value_w.astype(jnp.bfloat16), "dp", scatter_dimension=0, tiled=True
        ).astype(jnp.float32),
        lax.psum_scatter(
            grad_out_w.astype(jnp.bfloat16), "dp", scatter_dimension=1, tiled=True
        ).astype(jnp.float32),
    )
    first_gain_part = jnp.sum(grad_first * normed_first, axis=0)
    grad_tokens = grad_middle + rms_back(grad_first * first_gain_f, normed_first, inv_first)
    first_gain_sum, second_gain_sum = lax.psum(
        (first_gain_part, second_gain_part), ("dp", "tensor")
    )
    width = attn_gain.shape[0]
    dp_rank = lax.axis_index("dp")
    first_gain_grad = lax.dynamic_slice_in_dim(first_gain_sum, dp_rank * width, width)
    second_gain_grad = lax.dynamic_slice_in_dim(second_gain_sum, dp_rank * width, width)
    return (
        output[None],
        grad_tokens[None],
        first_gain_grad,
        grad_query_w,
        grad_key_w,
        grad_value_w,
        grad_out_w,
        second_gain_grad,
        grad_gate_w,
        grad_up_w,
        grad_down_w,
    )


def solution(mesh):
    return jax.shard_map(
        body,
        mesh=mesh,
        in_specs=(
            P("dp", "tensor", None),
            P("dp"),
            P("dp"),
            P("dp", "tensor"),
            P("dp", "tensor"),
            P("dp", "tensor"),
            P("tensor", "dp"),
            P("dp"),
            P("dp", "tensor"),
            P("dp", "tensor"),
            P("tensor", "dp"),
            P("dp", "tensor", None),
        ),
        out_specs=(
            P("dp", "tensor", None),
            P("dp", "tensor", None),
            P("dp"),
            P("dp", "tensor"),
            P("dp", "tensor"),
            P("dp", "tensor"),
            P("tensor", "dp"),
            P("dp"),
            P("dp", "tensor"),
            P("dp", "tensor"),
            P("tensor", "dp"),
        ),
        check_vma=False,
    )
```

profile of v0, /device:TPU:0, one launch (start us, length us, event | category | flops | bytes accessed | tf_op | source)
XLA Modules:
  0.0 1172.5 jit_solution(16675903397976520684)
XLA Ops:
  12.3 15.5 %all-reduce.5 = (bf16[1536]{0:T(1024)(128)(2,1)S(1)}, bf16[1536]{0:T(1024)(128)(2,1)S(1)}) all-reduce(bf16[1536]{0:T(1024)(128)(2,1)S(1)} %dynamic-update-slice.10, bf16[1536]{0:T(1024)(128)(2,1)S(1)} %dynamic-update-slice.11), channel_id=1, replica_groups=mesh['dp'=8,'tensor'=4] {'dp'}, use_global_device_ids=true, to_apply=%add.2 | all-reduce | flops 3072 | bytes 12288
  27.8 2.3 fusion.19
  33.5 9.4 all_gather.49
  42.9 10.4 all_gather.48
  53.6 39.4 %all-gather.10.cloned.1.call-done = bf16[1024,1536]{1,0:T(8,128)(2,1)} async-done(((bf16[256,1536]{1,0:T(8,128)(2,1)}), bf16[1024,1536]{1,0:T(8,128)(2,1)}) %all-gather.10.cloned.1.call-update) | async-done | bytes 3145744 | tf_op jit(solution)/shard_map/all_gather | solution.py:109
  93.0 3.2 convolution_convert_fusion.11
  98.4 19.2 %all-gather.12.cloned.1.call-done = bf16[1536,384]{1,0:T(8,128)(2,1)} async-done(((bf16[192,384]{1,0:T(8,128)(2,1)}), bf16[1536,384]{1,0:T(8,128)(2,1)}) %all-gather.12.cloned.1.call-update) | async-done | bytes 1179664 | tf_op jit(solution)/shard_map/all_gather | solution.py:96
  117.5 3.6 fusion.61
  129.5 2.5 convolution_convert_fusion.9
  132.0 11.4 all-gather.14.cloned.1.call-done
  143.4 5.8 fusion.34
  149.8 110.3 %reduce-scatter.12.cloned.1.call-done = f32[256,1536]{1,0:T(8,128)} async-done(((f32[1024,1536]{1,0:T(8,128)}), f32[256,1536]{1,0:T(8,128)}) %reduce-scatter.12.cloned.1.call-update) | async-done | bytes 1572880 | tf_op jit(solution)/shard_map/reduce_scatter | solution.py:149
  267.3 27.3 %all-gather.20.cloned.1.call-done = bf16[1536,1024]{1,0:T(8,128)(2,1)} async-done(((bf16[192,1024]{1,0:T(8,128)(2,1)}), bf16[1536,1024]{1,0:T(8,128)(2,1)}) %all-gather.20.cloned.1.call-update) | async-done | bytes 3145744 | tf_op jit(solution)/shard_map/all_gather | solution.py:158
  294.6 65.5 %all-gather.16.cloned.1.call-done = bf16[1024,1536]{1,0:T(8,128)(2,1)} async-done(((bf16[256,1536]{1,0:T(8,128)(2,1)}), bf16[1024,1536]{1,0:T(8,128)(2,1)}) %all-gather.16.cloned.1.call-update) | async-done | bytes 3145744 | tf_op jit(solution)/shard_map/all_gather | solution.py:166
  360.1 8.2 fusion.63
  368.3 24.5 %all-gather.18.cloned.1.call-done = bf16[1536,1024]{1,0:T(8,128)(2,1)} async-done(((bf16[192,1024]{1,0:T(8,128)(2,1)}), bf16[1536,1024]{1,0:T(8,128)(2,1)}) %all-gather.18.cloned.1.call-update) | async-done | bytes 3145744 | tf_op jit(solution)/shard_map/all_gather | solution.py:157
  392.8 8.2 fusion.62
  401.1 57.4 %all-gather.24.cloned.1.call-done = bf16[1024,1536]{1,0:T(8,128)(2,1)} async-done(((bf16[256,1536]{1,0:T(8,128)(2,1)}), bf16[1024,1536]{1,0:T(8,128)(2,1)}) %all-gather.24.cloned.1.call-update) | async-done | bytes 3145744 | tf_op jit(solution)/shard_map/all_gather | solution.py:188
  458.4 32.7 %all-gather.22.cloned.1.call-done = bf16[1024,1536]{0,1:T(8,128)(2,1)} async-done(((bf16[1024,192]{0,1:T(8,128)(2,1)}), bf16[1024,1536]{0,1:T(8,128)(2,1)}) %all-gather.22.cloned.1.call-update) | async-done | bytes 3145744 | tf_op jit(solution)/shard_map/all_gather | solution.py:159
  491.2 11.7 %multiply_convert_fusion = (bf16[1024,1024]{1,0:T(8,128)(2,1)S(1)}, bf16[1024,1024]{1,0:T(8,128)(2,1)S(1)}, bf16[1024,1024]{1,0:T(8,128)(2,1)}) fusion(f32[1024,1024]{1,0:T(8,128)} %fusion.62, f32[1024,1024]{1,0:T(8,128)} %fusion.63, bf16[1024,1536]{1,0:T(8,128)(2,1)} %all-gather.24.cloned.1.call-done, bf16[1024,1536]{0,1:T(8,128)(2,1)} %all-gather.22.cloned.1.call-done), kind=kOutput, calls=%fused_computation.18 | convolution fusion | flops 3238002688 | bytes 20971520 | tf_op jit(solution)/shard_map/dot_general | solution.py:43
  502.9 3.5 fusion.64
  506.4 5.7 convolution_add_fusion
  512.2 7.7 convolution_convert_fusion.3
  519.9 103.1 %reduce-scatter.16.cloned.1.call-done = f32[256,1536]{1,0:T(8,128)} async-done(((f32[1024,1536]{1,0:T(8,128)}), f32[256,1536]{1,0:T(8,128)}) %reduce-scatter.16.cloned.1.call-update) | async-done | bytes 1572880 | tf_op jit(solution)/shard_map/reduce_scatter | solution.py:195
  624.9 61.4 %reduce-scatter.14.cloned.1.call-done = bf16[256,1536]{1,0:T(8,128)(2,1)} async-done(((bf16[1024,1536]{1,0:T(8,128)(2,1)}), bf16[256,1536]{1,0:T(8,128)(2,1)}) %reduce-scatter.14.cloned.1.call-update) | async-done | bytes 786448 | tf_op jit(solution)/shard_map/reduce_scatter | solution.py:171
  686.3 4.4 fusion.57
  690.8 7.6 convolution_convert_fusion
  698.5 8.0 convolution_convert_fusion.1
  706.6 7.7 convolution_convert_fusion.2
  714.6 39.7 %all-gather.26.cloned.1.call-done = bf16[1024,1536]{1,0:T(8,128)(2,1)} async-done(((bf16[256,1536]{1,0:T(8,128)(2,1)}), bf16[1024,1536]{1,0:T(8,128)(2,1)}) %all-gather.26.cloned.1.call-update) | async-done | bytes 3145744 | tf_op jit(solution)/shard_map/all_gather | solution.py:216
  754.3 3.5 convolution_convert_fusion.8
  759.4 2.4 fusion.7
  764.7 2.5 fusion.29
  770.0 9.5 fusion
  780.0 7.1 fusion.2
  793.0 5.1 convolution_convert_fusion.4
  799.6 3.0 convolution_multiply_fusion
  804.5 2.9 convolution_convert_fusion.5
  810.8 2.7 add_convert_fusion
  815.7 36.0 %reduce-scatter.30.cloned.1.call-done = bf16[192,1024]{1,0:T(8,128)(2,1)} async-done(((bf16[1536,1024]{1,0:T(8,128)(2,1)}), bf16[192,1024]{1,0:T(8,128)(2,1)}) %reduce-scatter.30.cloned.1.call-update) | async-done | bytes 393232 | tf_op jit(solution)/shard_map/reduce_scatter | solution.py:207
  853.7 47.4 %reduce-scatter.28.cloned.1.call-done = bf16[192,1024]{1,0:T(8,128)(2,1)} async-done(((bf16[1536,1024]{1,0:T(8,128)(2,1)}), bf16[192,1024]{1,0:T(8,128)(2,1)}) %reduce-scatter.28.cloned.1.call-update) | async-done | bytes 393232 | tf_op jit(solution)/shard_map/reduce_scatter | solution.py:204
  903.1 36.0 %reduce-scatter.24.cloned.1.call-done = bf16[192,192]{1,0:T(8,128)(2,1)} async-done(((bf16[1536,192]{1,0:T(8,128)(2,1)}), bf16[192,192]{1,0:T(8,128)(2,1)}) %reduce-scatter.24.cloned.1.call-update) | async-done | bytes 73744 | tf_op jit(solution)/shard_map/reduce_scatter | solution.py:286
  940.7 36.4 %reduce-scatter.22.cloned.1.call-done = bf16[192,192]{1,0:T(8,128)(2,1)} async-done(((bf16[1536,192]{1,0:T(8,128)(2,1)}), bf16[192,192]{1,0:T(8,128)(2,1)}) %reduce-scatter.22.cloned.1.call-update) | async-done | bytes 73744 | tf_op jit(solution)/shard_map/reduce_scatter | solution.py:283
  978.6 38.2 %reduce-scatter.26.cloned.1.call-done = bf16[384,192]{0,1:T(8,128)(2,1)} async-done(((bf16[384,1536]{0,1:T(8,128)(2,1)}), bf16[384,192]{0,1:T(8,128)(2,1)}) %reduce-scatter.26.cloned.1.call-update) | async-done | bytes 147472 | tf_op jit(solution)/shard_map/reduce_scatter | solution.py:289
  1018.5 38.3 %reduce-scatter.20.cloned.1.call-done = bf16[192,384]{1,0:T(8,128)(2,1)} async-done(((bf16[1536,384]{1,0:T(8,128)(2,1)}), bf16[192,384]{1,0:T(8,128)(2,1)}) %reduce-scatter.20.cloned.1.call-update) | async-done | bytes 147472 | tf_op jit(solution)/shard_map/reduce_scatter | solution.py:280
  1058.5 60.9 %reduce-scatter.18.cloned.1.call-done = bf16[256,1536]{1,0:T(8,128)(2,1)} async-done(((bf16[1024,1536]{1,0:T(8,128)(2,1)}), bf16[256,1536]{1,0:T(8,128)(2,1)}) %reduce-scatter.18.cloned.1.call-update) | async-done | bytes 786448 | tf_op jit(solution)/shard_map/reduce_scatter | solution.py:266
  1121.2 40.3 %all-reduce.4 = (f32[1536]{0:T(1024)S(1)}, f32[1536]{0:T(1024)S(1)}) all-reduce(f32[1536]{0:T(1024)S(1)} %get-tuple-element.77, f32[1536]{0:T(1024)S(1)} %get-tuple-element.75), channel_id=1, replica_groups=mesh['dp'=8,'tensor'=4] {'dp','tensor'}, use_global_device_ids=true, to_apply=%region_15.16 | all-reduce | flops 3072 | bytes 24576 | tf_op jit(solution)/shard_map/psum | solution.py:295
  1162.8 2.7 fusion.18
  (208 shorter events, 63.4 us)
Async XLA Ops:
  7.2 26.4 %copy-start.42 = (bf16[192,192]{1,0:T(8,128)(2,1)S(1)}, bf16[192,192]{1,0:T(8,128)(2,1)}, u32[]{:S(2)}) copy-start(bf16[192,192]{1,0:T(8,128)(2,1)} %param.28) | copy-start | bytes 221188
  7.2 35.7 %copy-start.43 = (bf16[192,192]{1,0:T(8,128)(2,1)S(1)}, bf16[192,192]{1,0:T(8,128)(2,1)}, u32[]{:S(2)}) copy-start(bf16[192,192]{1,0:T(8,128)(2,1)} %param.29) | copy-start | bytes 221188
  7.2 85.8 %all-gather.10.cloned.1.call-start = ((), (), s32[]{:S(2)}) async-start(), calls=%async_computation.11 | async-start | bytes 3932160 | tf_op jit(solution)/shard_map/all_gather | solution.py:109
  8.7 24.9 %copy-start.44 = (f32[256]{0:T(256)}, f32[256]{0:T(256)S(1)}, u32[]{:S(2)}) copy-start(f32[256]{0:T(256)S(1)} %add_rsqrt_fusion.1) | copy-start | bytes 3076
  27.8 5.8 copy-start.40
  30.1 87.4 %all-gather.12.cloned.1.call-start = ((), (), s32[]{:S(2)}) async-start(), calls=%async_computation.12 | async-start | bytes 1327104 | tf_op jit(solution)/shard_map/all_gather | solution.py:96
  30.8 112.5 %all-gather.14.cloned.1.call-start = ((), (), s32[]{:S(2)}) async-start(), calls=%async_computation.13 | async-start | bytes 1327104 | tf_op jit(solution)/shard_map/all_gather | solution.py:99
  31.6 228.6 %reduce-scatter.12.cloned.1.call-start = ((), (), s32[]{:S(2)}) async-start(), calls=%async_computation.14 | async-start | bytes 7864320 | tf_op jit(solution)/shard_map/reduce_scatter | solution.py:149
  33.1 88.1 %copy-start.16 = (f32[1024,48]{0,1:T(8,128)}, f32[1024,48]{0,1:T(8,128)S(1)}, u32[]{:S(2)}) copy-start(f32[1024,48]{0,1:T(8,128)S(1)} %get-tuple-element.103) | copy-start | bytes 589828
  33.1 88.1 %copy-start.18 = (f32[1024,48]{0,1:T(8,128)}, f32[1024,48]{0,1:T(8,128)S(1)}, u32[]{:S(2)}) copy-start(f32[1024,48]{0,1:T(8,128)S(1)} %get-tuple-element.104) | copy-start | bytes 589828
  42.9 55.3 %copy-start.11 = (bf16[1536,192]{1,0:T(8,128)(2,1)}, bf16[1536,192]{1,0:T(8,128)(2,1)S(1)}, u32[]{:S(2)}) copy-start(bf16[1536,192]{1,0:T(8,128)(2,1)S(1)} %all_gather.49) | copy-start | bytes 1769476
  53.3 44.9 %copy-start.9 = (bf16[1536,192]{1,0:T(8,128)(2,1)}, bf16[1536,192]{1,0:T(8,128)(2,1)S(1)}, u32[]{:S(2)}) copy-start(bf16[1536,192]{1,0:T(8,128)(2,1)S(1)} %all_gather.48) | copy-start | bytes 1769476
  53.6 704.3 %copy-start.13 = (pred[512,512]{0,1:T(8,128)(4,1)}, pred[512,512]{0,1:T(8,128)(4,1)S(1)}, u32[]{:S(2)}) copy-start(pred[512,512]{0,1:T(8,128)(4,1)S(1)} %fusion.32) | copy-start | bytes 786436
  93.0 4.0 copy-start.5
  96.3 33.2 %copy-start.20 = (bf16[1024,192]{0,1:T(8,128)(2,1)}, bf16[1024,192]{0,1:T(8,128)(2,1)S(1)}, u32[]{:S(2)}) copy-start(bf16[1024,192]{0,1:T(8,128)(2,1)S(1)} %convolution_convert_fusion.11) | copy-start | bytes 1179652
  98.3 25.8 %copy-start.23 = (bf16[1024,2,48]{0,2,1:T(8,128)(2,1)}, bf16[1024,2,48]{0,2,1:T(8,128)(2,1)S(1)}, u32[]{:S(2)}) copy-start(bf16[1024,2,48]{0,2,1:T(8,128)(2,1)S(1)} %get-tuple-element.97) | copy-start | bytes 589828
  98.4 25.8 %copy-start.25 = (bf16[1024,2,48]{0,2,1:T(8,128)(2,1)}, bf16[1024,2,48]{0,2,1:T(8,128)(2,1)S(1)}, u32[]{:S(2)}) copy-start(bf16[1024,2,48]{0,2,1:T(8,128)(2,1)S(1)} %get-tuple-element.98) | copy-start | bytes 589828
  123.2 4.9 copy-start.1
  129.5 13.9 %copy-start.36 = (bf16[2,96,2,512]{3,1,2,0:T(8,128)(2,1)}, bf16[2,96,2,512]{3,1,2,0:T(8,128)(2,1)S(1)}, u32[]{:S(2)}) copy-start(bf16[2,96,2,512]{3,1,2,0:T(8,128)(2,1)S(1)} %convolution_convert_fusion.10) | copy-start | bytes 1179652
  132.0 17.2 %copy-start.37 = (bf16[2,96,2,512]{3,1,2,0:T(8,128)(2,1)}, bf16[2,96,2,512]{3,1,2,0:T(8,128)(2,1)S(1)}, u32[]{:S(2)}) copy-start(bf16[2,96,2,512]{3,1,2,0:T(8,128)(2,1)S(1)} %convolution_convert_fusion.9) | copy-start | bytes 1179652
  149.2 111.0 %copy-start.4 = (bf16[1,256,1536]{2,1,0:T(8,128)(2,1)S(1)}, bf16[1,256,1536]{2,1,0:T(8,128)(2,1)}, u32[]{:S(2)}) copy-start(bf16[1,256,1536]{2,1,0:T(8,128)(2,1)} %param.24) | copy-start | bytes 2359300
  149.2 145.4 %all-gather.20.cloned.1.call-start = ((), (), s32[]{:S(2)}) async-start(), calls=%async_computation.17 | async-start | bytes 3538944 | tf_op jit(solution)/shard_map/all_gather | solution.py:158
  149.8 210.3 %all-gather.16.cloned.1.call-start = ((), (), s32[]{:S(2)}) async-start(), calls=%async_computation.15 | async-start | bytes 3932160 | tf_op jit(solution)/shard_map/all_gather | solution.py:166
  262.9 129.9 %all-gather.18.cloned.1.call-start = ((), (), s32[]{:S(2)}) async-start(), calls=%async_computation.16 | async-start | bytes 3538944 | tf_op jit(solution)/shard_map/all_gather | solution.py:157
  263.7 194.7 %all-gather.24.cloned.1.call-start = ((), (), s32[]{:S(2)}) async-start(), calls=%async_computation.20 | async-start | bytes 3932160 | tf_op jit(solution)/shard_map/all_gather | solution.py:188
  266.0 225.2 %all-gather.22.cloned.1.call-start = ((), (), s32[]{:S(2)}) async-start(), calls=%async_computation.18 | async-start | bytes 3538944 | tf_op jit(solution)/shard_map/all_gather | solution.py:159
  266.7 356.3 %reduce-scatter.16.cloned.1.call-start = ((), (), s32[]{:S(2)}) async-start(), calls=%async_computation.21 | async-start | bytes 7864320 | tf_op jit(solution)/shard_map/reduce_scatter | solution.py:195
  491.2 11.7 %copy-start.47 = (bf16[1536,1024]{1,0:T(8,128)(2,1)S(1)}, bf16[1536,1024]{1,0:T(8,128)(2,1)}, u32[]{:S(2)}) copy-start(bf16[1536,1024]{1,0:T(8,128)(2,1)} %all-gather.18.cloned.1.call-done) | copy-start | bytes 9437188
  512.1 174.2 %reduce-scatter.14.cloned.1.call-start = ((), (), s32[]{:S(2)}) async-start(), calls=%async_computation.19 | async-start | bytes 3932160 | tf_op jit(solution)/shard_map/reduce_scatter | solution.py:171
  519.9 234.4 %all-gather.26.cloned.1.call-start = ((), (), s32[]{:S(2)}) async-start(), calls=%async_computation.22 | async-start | bytes 3932160 | tf_op jit(solution)/shard_map/all_gather | solution.py:216
  690.8 122.9 %reduce-scatter.32.cloned.1.call-start = ((), (), s32[]{:S(2)}) async-start(), calls=%async_computation.30 | async-start | bytes 3538944 | tf_op jit(solution)/shard_map/reduce_scatter | solution.py:210
  698.5 153.3 %reduce-scatter.30.cloned.1.call-start = ((), (), s32[]{:S(2)}) async-start(), calls=%async_computation.29 | async-start | bytes 3538944 | tf_op jit(solution)/shard_map/reduce_scatter | solution.py:207
  706.6 194.5 %reduce-scatter.28.cloned.1.call-start = ((), (), s32[]{:S(2)}) async-start(), calls=%async_computation.28 | async-start | bytes 3538944 | tf_op jit(solution)/shard_map/reduce_scatter | solution.py:204
  714.3 39.9 %copy-start.34 = (bf16[384,1536]{0,1:T(8,128)(2,1)S(1)}, bf16[384,1536]{0,1:T(8,128)(2,1)}, u32[]{:S(2)}) copy-start(bf16[384,1536]{0,1:T(8,128)(2,1)} %all-gather.14.cloned.1.call-done) | copy-start | bytes 3538948
  714.4 224.7 %reduce-scatter.24.cloned.1.call-start = ((), (), s32[]{:S(2)}) async-start(), calls=%async_computation.26 | async-start | bytes 884736 | tf_op jit(solution)/shard_map/reduce_scatter | solution.py:286
  757.8 6.9 copy-start.32
  757.8 6.8 slice-start
  759.4 5.3 slice-start.1
  779.5 197.5 %reduce-scatter.22.cloned.1.call-start = ((), (), s32[]{:S(2)}) async-start(), calls=%async_computation.25 | async-start | bytes 884736 | tf_op jit(solution)/shard_map/reduce_scatter | solution.py:283
  780.0 7.1 copy-start.28
  780.0 7.1 copy-start.29
  792.9 5.3 copy-start.24
  792.9 223.9 %reduce-scatter.26.cloned.1.call-start = ((), (), s32[]{:S(2)}) async-start(), calls=%async_computation.27 | async-start | bytes 1327104 | tf_op jit(solution)/shard_map/reduce_scatter | solution.py:289
  798.1 258.7 %reduce-scatter.20.cloned.1.call-start = ((), (), s32[]{:S(2)}) async-start(), calls=%async_computation.24 | async-start | bytes 1327104 | tf_op jit(solution)/shard_map/reduce_scatter | solution.py:280
  807.4 312.0 %reduce-scatter.18.cloned.1.call-start = ((), (), s32[]{:S(2)}) async-start(), calls=%async_computation.23 | async-start | bytes 3932160 | tf_op jit(solution)/shard_map/reduce_scatter | solution.py:266
  813.6 305.8 %copy-start.41 = (f32[1536]{0:T(1024)S(1)}, f32[1536]{0:T(1024)}, u32[]{:S(2)}) copy-start(f32[1536]{0:T(1024)} %copy-done.40) | copy-start | bytes 18436
  813.6 305.8 %copy-start.45 = (f32[256]{0:T(256)S(1)}, f32[256]{0:T(256)}, u32[]{:S(2)}) copy-start(f32[256]{0:T(256)} %copy-done.44) | copy-start | bytes 3076
  813.6 349.2 %copy-start.15 = (f32[256,1536]{1,0:T(8,128)S(1)}, f32[256,1536]{1,0:T(8,128)}, u32[]{:S(2)}) copy-start(f32[256,1536]{1,0:T(8,128)} %get-tuple-element.84) | copy-start | bytes 4718596
  (24 other events, 57.9 us)
Sparse Core Ops, SparseCore 0:
  30.2 62.7 all-gather.9
  94.9 22.5 all-gather.11
  119.4 23.9 all-gather.13
  149.3 110.7 reduce-scatter.11
  261.9 32.6 all-gather.19
  296.6 63.4 all-gather.15
  362.0 30.8 all-gather.17
  395.0 63.4 all-gather.23
  460.3 30.8 all-gather.21
  512.3 110.7 reduce-scatter.15
  625.4 60.8 reduce-scatter.13
  690.9 63.3 all-gather.25
  757.7 44.7 reduce-scatter.31
  805.7 46.0 reduce-scatter.29
  855.0 46.0 reduce-scatter.27
  904.1 34.9 reduce-scatter.23
  942.1 34.9 reduce-scatter.21
  980.1 36.6 reduce-scatter.25
  1020.1 36.6 reduce-scatter.19
  1059.0 60.3 reduce-scatter.17
where the time goes:
time: 1180 us; the launch traced here: 1170 us
  waiting for transfers between devices  889 us (75%)
  matrix products  132 us (11%)
  blocking collectives  75.5 us (6%)
  other arithmetic  46.9 us (4%)
  between operations  16.7 us (1%)
    reduce_scatter x1, waiting for transfers between devices, body(): lax.psum_scatter(jnp.dot(attended, out_full, preferred_element_type=jnp.f...  110 us
    reduce_scatter x1, waiting for transfers between devices, body(): lax.psum_scatter(transposed(grad_gate_low, gate_full) + transposed(grad_u...  103 us
    all_gather x1, waiting for transfers between devices, body(): second_all = lax.all_gather(second_low, 'tensor', axis=0, tiled=True)  65.5 us
    reduce_scatter x1, waiting for transfers between devices, body(): lax.psum_scatter(jnp.dot(hidden, down_full, preferred_element_type=jnp.fl...  61.4 us
    reduce_scatter x1, waiting for transfers between devices, body(): lax.psum_scatter((transposed(grad_query_proj, query_full) + transposed(gr...  60.9 us
    all_gather x1, waiting for transfers between devices, body(): lax.all_gather(grad_result.astype(jnp.bfloat16), 'tensor', axis=0, tiled=...  57.4 us
    reduce_scatter x1, waiting for transfers between devices, body(): lax.psum_scatter(grad_gate_w.astype(jnp.bfloat16), 'dp', scatter_dimensio...  47.4 us
    psum x1, blocking collectives, body(): lax.psum((first_gain_part, second_gain_part), ('dp', 'tensor'))  40.3 us
  transfers between devices with their start and end apart: 20, of which 19 were waited for; matrix products, arithmetic and copies ran while one was open for 12% of the time, Pallas kernels for 0%

commit v1 on v0

--- a/solution.py
+++ b/solution.py
@@ -185,7 +185,17 @@
         lax.all_gather(w_down, "dp", axis=1, tiled=True),
     )
     grad_result = jnp.where(own_valid, cotangent[0].astype(jnp.float32), 0.0)
-    grad_mlp_all = lax.all_gather(grad_result.astype(jnp.bfloat16), "tensor", axis=0, tiled=True)
+    x = grad_result.astype(jnp.bfloat16)
+    ways = lax.axis_size("tensor")
+    up = [(d, (d + 1) % ways) for d in range(ways)]
+    down = [(d, (d - 1) % ways) for d in range(ways)]
+    earlier, later = ([x], [x])
+    for _ in range(ways // 2):
+        earlier.append(lax.ppermute(earlier[-1], "tensor", up))
+    for _ in range((ways - 1) // 2):
+        later.append(lax.ppermute(later[-1], "tensor", down))
+    line = jnp.concatenate([*earlier[::-1], *later[1:]], axis=0)
+    grad_mlp_all = jnp.roll(line, (lax.axis_index("tensor") - ways // 2) * x.shape[0], axis=0)
     grad_down_w = outer_sum(hidden, grad_mlp_all)
     grad_hidden = transposed(grad_mlp_all, down_full)
     grad_gate_low = (

time: 1180 us -> 1130 us (0.958)
  waiting for transfers between devices: 889 us -> 820 us
  local copies, waits for them, and re-layouts: 10.6 us -> 23.1 us
    ppermute x0 -> x3, waiting for transfers between devices: none -> 78.1 us  [the longest x1 39.2 us: body(): later.append(lax.ppermute(later[-1], 'tensor', down))]
    all_gather x1 -> x0, waiting for transfers between devices: 57.4 us -> none  [body(): lax.all_gather(grad_result.astype(jnp.bfloat16), 'tensor', axis=0, tiled=...]
    all_gather x1, waiting for transfers between devices: 65.5 us -> 10.5 us  [body(): second_all = lax.all_gather(second_low, 'tensor', axis=0, tiled=True)]
    all_gather x1, waiting for transfers between devices: 27.3 us -> 0.01 us  [body(): lax.all_gather(w_up, 'dp', axis=0, tiled=True)]
  transfers between devices with their start and end apart: 20 -> 22, of which waited for: 19 -> 20; matrix products, arithmetic and copies ran while one was open for 12% -> 14% of each run, Pallas kernels for 0% -> 0%
where the time goes in v1:
time: 1130 us; the launch traced here: 1120 us
  waiting for transfers between devices  820 us (73%)
  matrix products  132 us (12%)
  blocking collectives  75.5 us (7%)
  other arithmetic  49.3 us (4%)
  local copies, waits for them, and re-layouts  23.1 us (2%)
  between operations  16.7 us (1%)
    reduce_scatter x1, waiting for transfers between devices, body(): lax.psum_scatter(jnp.dot(attended, out_full, preferred_element_type=jnp.f...  110 us
    reduce_scatter x1, waiting for transfers between devices, body(): lax.psum_scatter(transposed(grad_gate_low, gate_full) + transposed(grad_u...  103 us
    reduce_scatter x1, waiting for transfers between devices, body(): lax.psum_scatter(jnp.dot(hidden, down_full, preferred_element_type=jnp.fl...  61.2 us
    reduce_scatter x1, waiting for transfers between devices, body(): lax.psum_scatter((transposed(grad_query_proj, query_full) + transposed(gr...  61.1 us
    reduce_scatter x1, waiting for transfers between devices, body(): lax.psum_scatter(grad_gate_w.astype(jnp.bfloat16), 'dp', scatter_dimensio...  47.4 us
    psum x1, blocking collectives, body(): lax.psum((first_gain_part, second_gain_part), ('dp', 'tensor'))  40.3 us
    all_gather x1, waiting for transfers between devices, body(): lax.all_gather(grad_middle.astype(jnp.bfloat16), 'tensor', axis=0, tiled=...  39.7 us
    all_gather x1, waiting for transfers between devices, body(): first_all = lax.all_gather(first_low, 'tensor', axis=0, tiled=True)  39.4 us
  transfers between devices with their start and end apart: 22, of which 20 were waited for; matrix products, arithmetic and copies ran while one was open for 14% of the time, Pallas kernels for 0%

profile of v1, /device:TPU:0, one launch (start us, length us, event | category | flops | bytes accessed | tf_op | source)
XLA Modules:
  0.0 1123.4 jit_solution(12158879838844376301)
XLA Ops:
  12.3 15.5 %all-reduce.5 = (bf16[1536]{0:T(1024)(128)(2,1)S(1)}, bf16[1536]{0:T(1024)(128)(2,1)S(1)}) all-reduce(bf16[1536]{0:T(1024)(128)(2,1)S(1)} %dynamic-update-slice.10, bf16[1536]{0:T(1024)(128)(2,1)S(1)} %dynamic-update-slice.11), channel_id=1, replica_groups=mesh['dp'=8,'tensor'=4] {'dp'}, use_global_device_ids=true, to_apply=%add.2 | all-reduce | flops 3072 | bytes 12288
  33.5 9.4 all_gather.46
  42.9 10.4 all_gather.45
  53.6 39.4 %all-gather.9.cloned.1.call-done = bf16[1024,1536]{1,0:T(8,128)(2,1)} async-done(((bf16[256,1536]{1,0:T(8,128)(2,1)}), bf16[1024,1536]{1,0:T(8,128)(2,1)}) %all-gather.9.cloned.1.call-update) | async-done | bytes 3145744 | tf_op jit(solution)/shard_map/all_gather | solution.py:109
  93.0 3.2 convolution_convert_fusion.11
  98.4 19.2 %all-gather.11.cloned.1.call-done = bf16[1536,384]{1,0:T(8,128)(2,1)} async-done(((bf16[192,384]{1,0:T(8,128)(2,1)}), bf16[1536,384]{1,0:T(8,128)(2,1)}) %all-gather.11.cloned.1.call-update) | async-done | bytes 1179664 | tf_op jit(solution)/shard_map/all_gather | solution.py:96
  117.5 3.6 fusion.66
  129.7 2.5 convolution_convert_fusion.9
  132.2 11.2 all-gather.13.cloned.1.call-done
  143.4 5.7 fusion.37
  149.8 110.3 %reduce-scatter.12.cloned.1.call-done = f32[256,1536]{1,0:T(8,128)} async-done(((f32[1024,1536]{1,0:T(8,128)}), f32[256,1536]{1,0:T(8,128)}) %reduce-scatter.12.cloned.1.call-update) | async-done | bytes 1572880 | tf_op jit(solution)/shard_map/reduce_scatter | solution.py:149
  267.5 19.8 %collective-permute-done = bf16[256,1536]{1,0:T(8,128)(2,1)} collective-permute-done((bf16[256,1536]{1,0:T(8,128)(2,1)}, bf16[256,1536]{1,0:T(8,128)(2,1)}, u32[]{:S(2)}, u32[]{:S(2)}) %collective-permute-start) | collective-permute-done | bytes 786464 | tf_op jit(solution)/shard_map/ppermute | solution.py:194
  287.3 4.0 collective-permute-start.2
  291.2 19.1 %collective-permute-done.1 = bf16[256,1536]{1,0:T(8,128)(2,1)} collective-permute-done((bf16[256,1536]{1,0:T(8,128)(2,1)}, bf16[256,1536]{1,0:T(8,128)(2,1)}, u32[]{:S(2)}, u32[]{:S(2)}) %collective-permute-start.1) | collective-permute-done | bytes 786464 | tf_op jit(solution)/shard_map/ppermute | solution.py:194
  315.6 39.2 %collective-permute-done.2 = bf16[256,1536]{1,0:T(8,128)(2,1)} collective-permute-done((bf16[256,1536]{1,0:T(8,128)(2,1)}, bf16[256,1536]{1,0:T(8,128)(2,1)}, u32[]{:S(2)}, u32[]{:S(2)}) %collective-permute-start.2) | collective-permute-done | bytes 786464 | tf_op jit(solution)/shard_map/ppermute | solution.py:196
  364.3 10.5 all-gather.15.cloned.1.call-done
  374.8 8.2 fusion.68
  383.0 25.0 %all-gather.17.cloned.1.call-done = bf16[1536,1024]{1,0:T(8,128)(2,1)} async-done(((bf16[192,1024]{1,0:T(8,128)(2,1)}), bf16[1536,1024]{1,0:T(8,128)(2,1)}) %all-gather.17.cloned.1.call-update) | async-done | bytes 3145744 | tf_op jit(solution)/shard_map/all_gather | solution.py:157
  408.0 8.2 fusion.67
  416.2 25.8 %all-gather.21.cloned.1.call-done = bf16[1024,1536]{0,1:T(8,128)(2,1)} async-done(((bf16[1024,192]{0,1:T(8,128)(2,1)}), bf16[1024,1536]{0,1:T(8,128)(2,1)}) %all-gather.21.cloned.1.call-update) | async-done | bytes 3145744 | tf_op jit(solution)/shard_map/all_gather | solution.py:159
  442.1 11.6 %multiply_convert_fusion = (bf16[1024,1024]{1,0:T(8,128)(2,1)S(1)}, bf16[1024,1024]{1,0:T(8,128)(2,1)S(1)}, bf16[1024,1024]{1,0:T(8,128)(2,1)}) fusion(f32[1024,1024]{1,0:T(8,128)} %fusion.67, f32[1024,1024]{1,0:T(8,128)} %fusion.68, bf16[1024,1536]{0,1:T(8,128)(2,1)} %all-gather.21.cloned.1.call-done, ...), kind=kOutput, calls=%fused_computation.18 | convolution fusion | flops 3238002688 | bytes 20971524 | tf_op jit(solution)/shard_map/dot_general | solution.py:43
  453.7 3.5 fusion.69
  457.2 6.0 convolution_add_fusion
  463.3 7.7 convolution_convert_fusion.3
  471.0 103.1 %reduce-scatter.16.cloned.1.call-done = f32[256,1536]{1,0:T(8,128)} async-done(((f32[1024,1536]{1,0:T(8,128)}), f32[256,1536]{1,0:T(8,128)}) %reduce-scatter.16.cloned.1.call-update) | async-done | bytes 1572880 | tf_op jit(solution)/shard_map/reduce_scatter | solution.py:205
  576.1 61.2 %reduce-scatter.14.cloned.1.call-done = bf16[256,1536]{1,0:T(8,128)(2,1)} async-done(((bf16[1024,1536]{1,0:T(8,128)(2,1)}), bf16[256,1536]{1,0:T(8,128)(2,1)}) %reduce-scatter.14.cloned.1.call-update) | async-done | bytes 786448 | tf_op jit(solution)/shard_map/reduce_scatter | solution.py:171
  637.3 4.4 fusion.62
  641.8 7.7 convolution_convert_fusion
  649.6 8.0 convolution_convert_fusion.1
  657.7 7.6 convolution_convert_fusion.2
  665.6 39.7 %all-gather.23.cloned.1.call-done = bf16[1024,1536]{1,0:T(8,128)(2,1)} async-done(((bf16[256,1536]{1,0:T(8,128)(2,1)}), bf16[1024,1536]{1,0:T(8,128)(2,1)}) %all-gather.23.cloned.1.call-update) | async-done | bytes 3145744 | tf_op jit(solution)/shard_map/all_gather | solution.py:226
  705.3 3.5 convolution_convert_fusion.8
  715.7 2.5 fusion.32
  720.9 9.5 fusion
  730.8 7.1 fusion.2
  743.8 5.1 convolution_convert_fusion.4
  750.4 3.0 convolution_multiply_fusion
  755.3 2.9 convolution_convert_fusion.5
  761.7 2.8 add_convert_fusion
  766.7 36.1 %reduce-scatter.30.cloned.1.call-done = bf16[192,1024]{1,0:T(8,128)(2,1)} async-done(((bf16[1536,1024]{1,0:T(8,128)(2,1)}), bf16[192,1024]{1,0:T(8,128)(2,1)}) %reduce-scatter.30.cloned.1.call-update) | async-done | bytes 393232 | tf_op jit(solution)/shard_map/reduce_scatter | solution.py:217
  804.7 47.4 %reduce-scatter.28.cloned.1.call-done = bf16[192,1024]{1,0:T(8,128)(2,1)} async-done(((bf16[1536,1024]{1,0:T(8,128)(2,1)}), bf16[192,1024]{1,0:T(8,128)(2,1)}) %reduce-scatter.28.cloned.1.call-update) | async-done | bytes 393232 | tf_op jit(solution)/shard_map/reduce_scatter | solution.py:214
  854.0 36.0 %reduce-scatter.24.cloned.1.call-done = bf16[192,192]{1,0:T(8,128)(2,1)} async-done(((bf16[1536,192]{1,0:T(8,128)(2,1)}), bf16[192,192]{1,0:T(8,128)(2,1)}) %reduce-scatter.24.cloned.1.call-update) | async-done | bytes 73744 | tf_op jit(solution)/shard_map/reduce_scatter | solution.py:296
  891.6 36.4 %reduce-scatter.22.cloned.1.call-done = bf16[192,192]{1,0:T(8,128)(2,1)} async-done(((bf16[1536,192]{1,0:T(8,128)(2,1)}), bf16[192,192]{1,0:T(8,128)(2,1)}) %reduce-scatter.22.cloned.1.call-update) | async-done | bytes 73744 | tf_op jit(solution)/shard_map/reduce_scatter | solution.py:293
  929.6 38.2 %reduce-scatter.26.cloned.1.call-done = bf16[384,192]{0,1:T(8,128)(2,1)} async-done(((bf16[384,1536]{0,1:T(8,128)(2,1)}), bf16[384,192]{0,1:T(8,128)(2,1)}) %reduce-scatter.26.cloned.1.call-update) | async-done | bytes 147472 | tf_op jit(solution)/shard_map/reduce_scatter | solution.py:299
  969.4 38.2 %reduce-scatter.20.cloned.1.call-done = bf16[192,384]{1,0:T(8,128)(2,1)} async-done(((bf16[1536,384]{1,0:T(8,128)(2,1)}), bf16[192,384]{1,0:T(8,128)(2,1)}) %reduce-scatter.20.cloned.1.call-update) | async-done | bytes 147472 | tf_op jit(solution)/shard_map/reduce_scatter | solution.py:290
  1009.2 61.1 %reduce-scatter.18.cloned.1.call-done = bf16[256,1536]{1,0:T(8,128)(2,1)} async-done(((bf16[1024,1536]{1,0:T(8,128)(2,1)}), bf16[256,1536]{1,0:T(8,128)(2,1)}) %reduce-scatter.18.cloned.1.call-update) | async-done | bytes 786448 | tf_op jit(solution)/shard_map/reduce_scatter | solution.py:276
  1072.1 40.3 %all-reduce.4 = (f32[1536]{0:T(1024)S(1)}, f32[1536]{0:T(1024)S(1)}) all-reduce(f32[1536]{0:T(1024)S(1)} %get-tuple-element.77, f32[1536]{0:T(1024)S(1)} %get-tuple-element.75), channel_id=1, replica_groups=mesh['dp'=8,'tensor'=4] {'dp','tensor'}, use_global_device_ids=true, to_apply=%region_15.16 | all-reduce | flops 3072 | bytes 24576 | tf_op jit(solution)/shard_map/psum | solution.py:305
  1113.7 2.7 fusion.21
  (221 shorter events, 83.1 us)
Async XLA Ops:
  7.2 26.4 %copy-start.43 = (bf16[192,192]{1,0:T(8,128)(2,1)S(1)}, bf16[192,192]{1,0:T(8,128)(2,1)}, u32[]{:S(2)}) copy-start(bf16[192,192]{1,0:T(8,128)(2,1)} %param.28) | copy-start | bytes 221188
  7.2 35.7 %copy-start.44 = (bf16[192,192]{1,0:T(8,128)(2,1)S(1)}, bf16[192,192]{1,0:T(8,128)(2,1)}, u32[]{:S(2)}) copy-start(bf16[192,192]{1,0:T(8,128)(2,1)} %param.29) | copy-start | bytes 221188
  7.2 85.8 %all-gather.9.cloned.1.call-start = ((), (), s32[]{:S(2)}) async-start(), calls=%async_computation.11 | async-start | bytes 3932160 | tf_op jit(solution)/shard_map/all_gather | solution.py:109
  8.7 24.9 %copy-start.45 = (f32[256]{0:T(256)}, f32[256]{0:T(256)S(1)}, u32[]{:S(2)}) copy-start(f32[256]{0:T(256)S(1)} %add_rsqrt_fusion.1) | copy-start | bytes 3076
  27.8 5.8 copy-start.41
  30.1 87.4 %all-gather.11.cloned.1.call-start = ((), (), s32[]{:S(2)}) async-start(), calls=%async_computation.12 | async-start | bytes 1327104 | tf_op jit(solution)/shard_map/all_gather | solution.py:96
  30.8 112.5 %all-gather.13.cloned.1.call-start = ((), (), s32[]{:S(2)}) async-start(), calls=%async_computation.13 | async-start | bytes 1327104 | tf_op jit(solution)/shard_map/all_gather | solution.py:99
  31.6 228.5 %reduce-scatter.12.cloned.1.call-start = ((), (), s32[]{:S(2)}) async-start(), calls=%async_computation.14 | async-start | bytes 7864320 | tf_op jit(solution)/shard_map/reduce_scatter | solution.py:149
  33.1 88.1 %copy-start.17 = (f32[1024,48]{0,1:T(8,128)}, f32[1024,48]{0,1:T(8,128)S(1)}, u32[]{:S(2)}) copy-start(f32[1024,48]{0,1:T(8,128)S(1)} %get-tuple-element.103) | copy-start | bytes 589828
  33.1 88.1 %copy-start.19 = (f32[1024,48]{0,1:T(8,128)}, f32[1024,48]{0,1:T(8,128)S(1)}, u32[]{:S(2)}) copy-start(f32[1024,48]{0,1:T(8,128)S(1)} %get-tuple-element.104) | copy-start | bytes 589828
  42.9 55.3 %copy-start.12 = (bf16[1536,192]{1,0:T(8,128)(2,1)}, bf16[1536,192]{1,0:T(8,128)(2,1)S(1)}, u32[]{:S(2)}) copy-start(bf16[1536,192]{1,0:T(8,128)(2,1)S(1)} %all_gather.46) | copy-start | bytes 1769476
  53.3 44.9 %copy-start.10 = (bf16[1536,192]{1,0:T(8,128)(2,1)}, bf16[1536,192]{1,0:T(8,128)(2,1)S(1)}, u32[]{:S(2)}) copy-start(bf16[1536,192]{1,0:T(8,128)(2,1)S(1)} %all_gather.45) | copy-start | bytes 1769476
  53.6 655.2 %copy-start.14 = (pred[512,512]{0,1:T(8,128)(4,1)}, pred[512,512]{0,1:T(8,128)(4,1)S(1)}, u32[]{:S(2)}) copy-start(pred[512,512]{0,1:T(8,128)(4,1)S(1)} %fusion.35) | copy-start | bytes 786436
  96.3 33.4 %copy-start.21 = (bf16[1024,192]{0,1:T(8,128)(2,1)}, bf16[1024,192]{0,1:T(8,128)(2,1)S(1)}, u32[]{:S(2)}) copy-start(bf16[1024,192]{0,1:T(8,128)(2,1)S(1)} %convolution_convert_fusion.11) | copy-start | bytes 1179652
  98.3 25.8 %copy-start.24 = (bf16[1024,2,48]{0,2,1:T(8,128)(2,1)}, bf16[1024,2,48]{0,2,1:T(8,128)(2,1)S(1)}, u32[]{:S(2)}) copy-start(bf16[1024,2,48]{0,2,1:T(8,128)(2,1)S(1)} %get-tuple-element.97) | copy-start | bytes 589828
  98.4 25.8 %copy-start.26 = (bf16[1024,2,48]{0,2,1:T(8,128)(2,1)}, bf16[1024,2,48]{0,2,1:T(8,128)(2,1)S(1)}, u32[]{:S(2)}) copy-start(bf16[1024,2,48]{0,2,1:T(8,128)(2,1)S(1)} %get-tuple-element.98) | copy-start | bytes 589828
  129.7 13.7 %copy-start.37 = (bf16[2,96,2,512]{3,1,2,0:T(8,128)(2,1)}, bf16[2,96,2,512]{3,1,2,0:T(8,128)(2,1)S(1)}, u32[]{:S(2)}) copy-start(bf16[2,96,2,512]{3,1,2,0:T(8,128)(2,1)S(1)} %convolution_convert_fusion.10) | copy-start | bytes 1179652
  132.2 16.9 %copy-start.38 = (bf16[2,96,2,512]{3,1,2,0:T(8,128)(2,1)}, bf16[2,96,2,512]{3,1,2,0:T(8,128)(2,1)S(1)}, u32[]{:S(2)}) copy-start(bf16[2,96,2,512]{3,1,2,0:T(8,128)(2,1)S(1)} %convolution_convert_fusion.9) | copy-start | bytes 1179652
  149.1 111.0 %copy-start.4 = (bf16[1,256,1536]{2,1,0:T(8,128)(2,1)S(1)}, bf16[1,256,1536]{2,1,0:T(8,128)(2,1)}, u32[]{:S(2)}) copy-start(bf16[1,256,1536]{2,1,0:T(8,128)(2,1)} %param.24) | copy-start | bytes 2359300
  149.1 215.1 %all-gather.19.cloned.1.call-start = ((), (), s32[]{:S(2)}) async-start(), calls=%async_computation.17 | async-start | bytes 3538944 | tf_op jit(solution)/shard_map/all_gather | solution.py:158
  149.7 225.1 %all-gather.15.cloned.1.call-start = ((), (), s32[]{:S(2)}) async-start(), calls=%async_computation.15 | async-start | bytes 3932160 | tf_op jit(solution)/shard_map/all_gather | solution.py:166
  262.9 145.1 %all-gather.17.cloned.1.call-start = ((), (), s32[]{:S(2)}) async-start(), calls=%async_computation.16 | async-start | bytes 3538944 | tf_op jit(solution)/shard_map/all_gather | solution.py:157
  263.6 178.5 %all-gather.21.cloned.1.call-start = ((), (), s32[]{:S(2)}) async-start(), calls=%async_computation.18 | async-start | bytes 3538944 | tf_op jit(solution)/shard_map/all_gather | solution.py:159
  265.9 21.3 %collective-permute-start = (bf16[256,1536]{1,0:T(8,128)(2,1)}, bf16[256,1536]{1,0:T(8,128)(2,1)}, u32[]{:S(2)}, u32[]{:S(2)}) collective-permute-start(bf16[256,1536]{1,0:T(8,128)(2,1)} %fusion.27), channel_id=1, source_target_pairs={{0,1},{1,2},{2,3},{3,0},{4,5},{5,6},{6,7},{7,4},{8,9},{9,10},{10,1... | collective-permute-start | bytes 2359304 | tf_op jit(solution)/shard_map/ppermute | solution.py:194
  267.4 306.8 %reduce-scatter.16.cloned.1.call-start = ((), (), s32[]{:S(2)}) async-start(), calls=%async_computation.20 | async-start | bytes 7864320 | tf_op jit(solution)/shard_map/reduce_scatter | solution.py:205
  287.3 23.1 %collective-permute-start.1 = (bf16[256,1536]{1,0:T(8,128)(2,1)}, bf16[256,1536]{1,0:T(8,128)(2,1)}, u32[]{:S(2)}, u32[]{:S(2)}) collective-permute-start(bf16[256,1536]{1,0:T(8,128)(2,1)} %collective-permute-done), channel_id=1, source_target_pairs={{0,1},{1,2},{2,3},{3,0},{4,5},{5,6},{6,7},{7,4},{8,9},{9,10},{10,1... | collective-permute-start | bytes 2359304 | tf_op jit(solution)/shard_map/ppermute | solution.py:194
  287.3 67.6 %collective-permute-start.2 = (bf16[256,1536]{1,0:T(8,128)(2,1)}, bf16[256,1536]{1,0:T(8,128)(2,1)}, u32[]{:S(2)}, u32[]{:S(2)}) collective-permute-start(bf16[256,1536]{1,0:T(8,128)(2,1)} %fusion.27), channel_id=1, source_target_pairs={{0,3},{1,0},{2,1},{3,2},{4,7},{5,4},{6,5},{7,6},{8,11},{9,8},{10,9... | collective-permute-start | bytes 2359304 | tf_op jit(solution)/shard_map/ppermute | solution.py:196
  291.2 23.3 %copy-start.9 = (bf16[1,256,1536]{2,1,0:T(8,128)(2,1)S(1)}, bf16[1,256,1536]{2,1,0:T(8,128)(2,1)}, u32[]{:S(2)}) copy-start(bf16[1,256,1536]{2,1,0:T(8,128)(2,1)} %param.35) | copy-start | bytes 2359300
  442.1 11.6 %copy-start.48 = (bf16[1536,1024]{1,0:T(8,128)(2,1)S(1)}, bf16[1536,1024]{1,0:T(8,128)(2,1)}, u32[]{:S(2)}) copy-start(bf16[1536,1024]{1,0:T(8,128)(2,1)} %all-gather.17.cloned.1.call-done) | copy-start | bytes 9437188
  463.3 174.0 %reduce-scatter.14.cloned.1.call-start = ((), (), s32[]{:S(2)}) async-start(), calls=%async_computation.19 | async-start | bytes 3932160 | tf_op jit(solution)/shard_map/reduce_scatter | solution.py:171
  471.0 234.3 %all-gather.23.cloned.1.call-start = ((), (), s32[]{:S(2)}) async-start(), calls=%async_computation.21 | async-start | bytes 3932160 | tf_op jit(solution)/shard_map/all_gather | solution.py:226
  641.8 122.8 %reduce-scatter.32.cloned.1.call-start = ((), (), s32[]{:S(2)}) async-start(), calls=%async_computation.29 | async-start | bytes 3538944 | tf_op jit(solution)/shard_map/reduce_scatter | solution.py:220
  649.5 153.2 %reduce-scatter.30.cloned.1.call-start = ((), (), s32[]{:S(2)}) async-start(), calls=%async_computation.28 | async-start | bytes 3538944 | tf_op jit(solution)/shard_map/reduce_scatter | solution.py:217
  657.6 194.4 %reduce-scatter.28.cloned.1.call-start = ((), (), s32[]{:S(2)}) async-start(), calls=%async_computation.27 | async-start | bytes 3538944 | tf_op jit(solution)/shard_map/reduce_scatter | solution.py:214
  665.3 39.9 %copy-start.35 = (bf16[384,1536]{0,1:T(8,128)(2,1)S(1)}, bf16[384,1536]{0,1:T(8,128)(2,1)}, u32[]{:S(2)}) copy-start(bf16[384,1536]{0,1:T(8,128)(2,1)} %all-gather.13.cloned.1.call-done) | copy-start | bytes 3538948
  665.4 224.7 %reduce-scatter.24.cloned.1.call-start = ((), (), s32[]{:S(2)}) async-start(), calls=%async_computation.25 | async-start | bytes 884736 | tf_op jit(solution)/shard_map/reduce_scatter | solution.py:296
  708.8 6.9 copy-start.33
  708.8 6.8 slice-start
  710.4 5.3 slice-start.1
  730.5 197.5 %reduce-scatter.22.cloned.1.call-start = ((), (), s32[]{:S(2)}) async-start(), calls=%async_computation.24 | async-start | bytes 884736 | tf_op jit(solution)/shard_map/reduce_scatter | solution.py:293
  730.8 7.1 copy-start.29
  730.8 7.1 copy-start.30
  743.7 224.1 %reduce-scatter.26.cloned.1.call-start = ((), (), s32[]{:S(2)}) async-start(), calls=%async_computation.26 | async-start | bytes 1327104 | tf_op jit(solution)/shard_map/reduce_scatter | solution.py:299
  748.9 258.7 %reduce-scatter.20.cloned.1.call-start = ((), (), s32[]{:S(2)}) async-start(), calls=%async_computation.23 | async-start | bytes 1327104 | tf_op jit(solution)/shard_map/reduce_scatter | solution.py:290
  758.2 312.1 %reduce-scatter.18.cloned.1.call-start = ((), (), s32[]{:S(2)}) async-start(), calls=%async_computation.22 | async-start | bytes 3932160 | tf_op jit(solution)/shard_map/reduce_scatter | solution.py:276
  764.5 305.8 %copy-start.42 = (f32[1536]{0:T(1024)S(1)}, f32[1536]{0:T(1024)}, u32[]{:S(2)}) copy-start(f32[1536]{0:T(1024)} %copy-done.41) | copy-start | bytes 18436
  764.5 305.8 %copy-start.46 = (f32[256]{0:T(256)S(1)}, f32[256]{0:T(256)}, u32[]{:S(2)}) copy-start(f32[256]{0:T(256)} %copy-done.45) | copy-start | bytes 3076
  764.5 349.1 %copy-start.16 = (f32[256,1536]{1,0:T(8,128)S(1)}, f32[256,1536]{1,0:T(8,128)}, u32[]{:S(2)}) copy-start(f32[256,1536]{1,0:T(8,128)} %get-tuple-element.84) | copy-start | bytes 4718596
  (27 other events, 72.7 us)
Sparse Core Ops, SparseCore 0:
  30.2 62.7 all-gather.8
  94.9 22.5 all-gather.10
  119.4 23.9 all-gather.12
  149.3 110.7 reduce-scatter.11
  261.8 32.6 all-gather.18
  296.5 78.2 all-gather.14
  376.7 31.2 all-gather.16
  409.9 32.1 all-gather.20
  463.4 110.7 reduce-scatter.15
  576.3 60.9 reduce-scatter.13
  641.9 63.3 all-gather.22
  708.5 44.6 reduce-scatter.31
  756.6 46.0 reduce-scatter.29
  806.0 46.0 reduce-scatter.27
  855.1 34.9 reduce-scatter.23
  893.0 34.9 reduce-scatter.21
  931.1 36.6 reduce-scatter.25
  970.9 36.6 reduce-scatter.19
  1009.9 60.3 reduce-scatter.17
